TPU v7x, 32 devices: a whole 2x2x4 slice. The times are simulated.
32 devices in a mesh: dom: 32 (over z, y, x, core).
Axes of the slice: x: 2, y: 2, z: 4, core: 2. Of those that a mesh axis runs over, the one named last changes fastest.
Arguments:
- tracers: float32 [20, 8, 32768], P(None, None, 'dom'), may hold values from -6 to 6
- mass_flux: float32 [3, 8, 32768], P(None, None, 'dom'), may hold values from -6 to 6
- lsq_coeff: float32 [2, 3, 32768], P(None, None, 'dom'), may hold values from -3 to 3
- own_offset: float32 [2, 3, 8, 32768], P(None, None, None, 'dom'), may hold values from -1.5 to 1.5
- far_offset: float32 [2, 3, 8, 32768], P(None, None, None, 'dom'), may hold values from -1.5 to 1.5
- inv_mass: float32 [8, 32768], P(None, 'dom'), may hold values from 0.25 to 1
- neighbour: int32 [3, 32768], P(None, 'dom'), may hold values from 0 to 1791, as said below
- send_cells: int32 [6, 4096], P(None, 'dom'), may hold values from 0 to 1023, as said below
Outputs:
- updated: float32 [20, 8, 32768], P(None, None, 'dom')
Inputs may be any that keep to these rules, and one draw needn't show every extreme that they name: For each domain, entries index its 1024 own cells followed by 6 received blocks of 128 slots; every referenced received slot holds a real cell of the sending domain, the unused tail of a block is never referenced, and for every neighbour slot some domain references a block in full. `send_cells`: each block of 128 entries (one sending domain, one neighbour slot) lists distinct own cells of the sending domain, as local indices.
All inputs are finite; a program needn't handle non-finite values.
Results may differ from a plain program's by a relative error of at most 0.0003.
Values sent between devices are 32-bit elements; how exact they have to be, the bound alone decides.
A program may use at most 64 MiB of HBM per device.

v0:
```python
import functools

import jax
import jax.numpy as jnp
from jax import lax
from jax.experimental import pallas as pl
from jax.experimental.pallas import tpu as pltpu
from jax.sharding import PartitionSpec as P

MESH = pl.DeviceIdType.MESH
PARTS = (2, 3, 3, 2)
WIDTH = 1536


def peer_shift(peer_slot):
    return (peer_slot // 2 + 1) * (1 - 2 * (peer_slot % 2))


def lanes(block, width):
    return pl.ds(pl.multiple_of(block * width, width), width)


def split(value):
    high = value.astype(jnp.bfloat16)
    return high, (value - high.astype(jnp.float32)).astype(jnp.bfloat16)


def kernel(
    parts,
    tracers_hbm,
    flux_hbm,
    lsq_hbm,
    own_hbm,
    far_hbm,
    inv_hbm,
    near_hbm,
    send_hbm,
    out,
    tracers,
    flux,
    lsq,
    own_off,
    far_off,
    inv_mass,
    near,
    send_cells,
    load_sem,
    hot,
    send_hot,
    low_x,
    low_g,
    grads,
    beside,
    far,
    value_out,
    value_in,
    grad_out,
    grad_in,
    halo_x,
    halo_g,
    send_sem,
    recv_sem,
):
    tracer_count, level_count, cells = tracers.shape
    rows = tracer_count * level_count
    peers, halo = send_cells.shape
    ext = cells + peers * halo
    me = lax.axis_index("dom")
    devices = lax.axis_size("dom")
    target = [lax.rem(me + peer_shift(p) + devices, devices) for p in range(peers)]
    f32, bf16 = jnp.float32, jnp.bfloat16
    order = [p for q in (1, 2, 0) for p in range(peers) if p // 2 == q]
    order += [p for p in range(peers) if p not in order]

    barrier = pltpu.get_barrier_semaphore()
    for p in range(peers):
        pl.semaphore_signal(barrier, inc=1, device_id=(target[p],), device_id_type=MESH)

    pairs = (
        (send_hbm, send_cells),
        (tracers_hbm, tracers),
        (near_hbm, near),
        (lsq_hbm, lsq),
        (flux_hbm, flux),
        (own_hbm, own_off),
        (far_hbm, far_off),
        (inv_hbm, inv_mass),
    )
    loads = [pltpu.make_async_copy(a, b, load_sem.at[i]) for i, (a, b) in enumerate(pairs)]
    for load in loads:
        load.start()
    loads[0].wait()

    for p in range(peers):
        index = jnp.broadcast_to(send_cells[p : p + 1, :], (cells, halo))
        equal = lax.broadcasted_iota(jnp.int32, (cells, halo), 0) == index
        send_hot[:, p * halo : (p + 1) * halo] = jnp.where(equal, 1.0, 0.0).astype(bf16)

    loads[1].wait()

    def split_x(start, count):
        def step(i, carry):
            t = start // level_count + 2 * i
            high, low = split(jnp.concatenate([tracers[t], tracers[t + 1]], axis=0))
            base = 2 * start + 16 * i
            low_x[pl.ds(pl.multiple_of(base, 16), 16), :] = high
            low_x[pl.ds(pl.multiple_of(base + count, 16), 16), :] = low
            return carry

        lax.fori_loop(0, count // 16, step, 0)

    def copies(kind, c):
        src, dst = (value_out, value_in) if kind == 0 else (grad_out, grad_in)
        start, count = [(1 + kind) * v for v in parts[c]]
        return [
            pltpu.make_async_remote_copy(
                src_ref=src.at[p, pl.ds(start, count)],
                dst_ref=dst.at[p, pl.ds(start, count)],
                send_sem=send_sem.at[kind, c, p],
                recv_sem=recv_sem.at[kind, c, p],
                device_id=(target[p],),
                device_id_type=MESH,
            )
            for p in order
        ]

    def pack(terms, dest, start, count):
        for p in range(0, peers, 2):
            part = jnp.dot(
                terms[pl.ds(2 * start, 2 * count), :],
                send_hot[:, p * halo : (p + 2) * halo],
                preferred_element_type=f32,
            )
            part = part[:count] + part[count:]
            for q in range(2):
                dest[p + q, pl.ds(start, count), :] = part[:, q * halo : (q + 1) * halo]

    def local(terms, dest, scale):
        def step(b, carry):
            cols = lanes(b, WIDTH)
            part = jnp.dot(terms[...], hot[:cells, cols], preferred_element_type=f32)
            for start, count in parts:
                start, count = scale * start, scale * count
                s = 2 * start
                dest[start : start + count, cols] = (
                    part[s : s + count] + part[s + count : s + 2 * count]
                )
            return carry

        lax.fori_loop(0, 3 * cells // WIDTH, step, 0)

    def remote(arrived, terms, dest, start, count):
        for p in range(peers):
            high, low = split(arrived[p, pl.ds(start, count), :])
            terms[:count, p * halo : (p + 1) * halo] = high
            terms[count : 2 * count, p * halo : (p + 1) * halo] = low

        def step(b, carry):
            cols = lanes(b, 2 * WIDTH)
            part = jnp.dot(
                terms[: 2 * count, :], hot[cells:ext, cols], preferred_element_type=f32
            )
            dest[start : start + count, cols] += part[:count] + part[count:]
            return carry

        lax.fori_loop(0, 3 * cells // (2 * WIDTH), step, 0)

    def gradient(start, per):
        def step(i, carry):
            t = start // level_count + 2 * i
            r = start + 16 * i
            here = jnp.concatenate([tracers[t], tracers[t + 1]], axis=0)
            at = pl.ds(pl.multiple_of(r, 16), 16)
            delta = [beside[at, j * cells : (j + 1) * cells] - here for j in range(3)]
            for k in range(2):
                total = lsq[0, k : k + 1, :] * delta[0]
                total = total + lsq[1, k : k + 1, :] * delta[1]
                total = total + lsq[2, k : k + 1, :] * delta[2]
                grads[k, at, :] = total
                high, low = split(total)
                base = 4 * start + k * per + 16 * i
                low_g[pl.ds(pl.multiple_of(base, 16), 16), :] = high
                low_g[pl.ds(pl.multiple_of(base + 2 * per, 16), 16), :] = low
            return carry

        lax.fori_loop(0, per // 16, step, 0)

    def finish(start, per):
        def step(i, carry):
            t = start // level_count + i
            at = pl.ds(pl.multiple_of(t * level_count, 8), level_count)
            f0 = pl.ds(pl.multiple_of(2 * start + i * level_count, 8), level_count)
            f1 = pl.ds(pl.multiple_of(2 * start + per + i * level_count, 8), level_count)
            for b in range(cells // 256):
                own = slice(b * 256, (b + 1) * 256)
                here = tracers[t, :, own]
                g0, g1 = grads[0, at, own], grads[1, at, own]
                outflow = None
                for j in range(3):
                    cols = slice(j * cells + b * 256, j * cells + (b + 1) * 256)
                    there = beside[at, cols]
                    own_face = here + g0 * own_off[0, j, :, own] + g1 * own_off[1, j, :, own]
                    far_face = (
                        there
                        + far[f0, cols] * far_off[0, j, :, own]
                        + far[f1, cols] * far_off[1, j, :, own]
                    )
                    side = flux[j, :, own]
                    face = jnp.where(side > 0, own_face, far_face)
                    face = jnp.maximum(face, jnp.minimum(here, there))
                    face = jnp.minimum(face, jnp.maximum(here, there))
                    term = side * face
                    outflow = term if outflow is None else outflow + term
                out[t, :, own] = here - inv_mass[:, own] * outflow
            return carry

        lax.fori_loop(0, per // level_count, step, 0)

    count_parts = len(parts)
    for part in parts:
        split_x(*part)
    whole = jnp.dot(low_x[...], send_hot[...], preferred_element_type=f32)
    for start, count in parts:
        part = whole[2 * start : 2 * start + count] + whole[2 * start + count : 2 * (start + count)]
        for p in range(peers):
            value_out[p, start : start + count, :] = part[:, p * halo : (p + 1) * halo]
    pl.semaphore_wait(barrier, peers)
    for c in range(count_parts):
        for copy in copies(0, c):
            copy.start()
    loads[2].wait()
    for j in range(3):

        def build(b, carry):
            cols = lanes(b, 128)
            index = jnp.broadcast_to(near[j : j + 1, cols], (ext, 128))
            equal = lax.broadcasted_iota(jnp.int32, (ext, 128), 0) == index
            hot[:, pl.ds(pl.multiple_of(j * cells + b * 128, 128), 128)] = jnp.where(
                equal, 1.0, 0.0
            ).astype(bf16)
            return carry

        lax.fori_loop(0, cells // 128, build, 0)

    local(low_x, beside, 1)
    loads[3].wait()
    for c in range(count_parts):
        start, count = parts[c]
        for copy in copies(0, c):
            copy.wait_recv()
        remote(value_in, halo_x, beside, start, count)
        gradient(start, count)
        pack(low_g, grad_out, 2 * start, 2 * count)
        for copy in copies(1, c):
            copy.start()
    local(low_g, far, 2)
    for load in loads[4:]:
        load.wait()
    for c in range(count_parts):
        start, count = parts[c]
        for copy in copies(1, c):
            copy.wait_recv()
        remote(grad_in, halo_g, far, 2 * start, 2 * count)
        finish(start, count)
    for kind in range(2):
        for c in range(count_parts):
            for copy in copies(kind, c):
                copy.wait_send()


def on_device(tracers, flux, lsq, own_off, far_off, inv_mass, near, send_cells):
    tracer_count, level_count, cells = tracers.shape
    rows = tracer_count * level_count
    peers, halo = send_cells.shape
    sizes = PARTS if 16 * sum(PARTS) == rows else (rows // 16,)
    parts, start = [], 0
    for size in sizes:
        parts.append((start, 16 * size))
        start += 16 * size
    per = 16 * max(sizes)
    lsq = lsq.transpose(1, 0, 2)
    operands = (tracers, flux, lsq, own_off, far_off, inv_mass, near, send_cells)
    ext = cells + peers * halo
    f32, bf16 = jnp.float32, jnp.bfloat16
    return pl.pallas_call(
        functools.partial(kernel, parts),
        out_shape=jax.ShapeDtypeStruct(tracers.shape, f32),
        in_specs=[pl.BlockSpec(memory_space=pltpu.HBM)] * 8,
        out_specs=pl.BlockSpec(memory_space=pltpu.VMEM),
        scratch_shapes=[pltpu.VMEM(a.shape, a.dtype) for a in operands]
        + [
            pltpu.SemaphoreType.DMA((8,)),
            pltpu.VMEM((ext, 3 * cells), bf16),
            pltpu.VMEM((cells, peers * halo), bf16),
            pltpu.VMEM((2 * rows, cells), bf16),
            pltpu.VMEM((4 * rows, cells), bf16),
            pltpu.VMEM((2, rows, cells), f32),
            pltpu.VMEM((rows, 3 * cells), f32),
            pltpu.VMEM((2 * rows, 3 * cells), f32),
            pltpu.VMEM((peers, rows, halo), f32),
            pltpu.VMEM((peers, rows, halo), f32),
            pltpu.VMEM((peers, 2 * rows, halo), f32),
            pltpu.VMEM((peers, 2 * rows, halo), f32),
            pltpu.VMEM((2 * per, peers * halo), bf16),
            pltpu.VMEM((4 * per, peers * halo), bf16),
            pltpu.SemaphoreType.DMA((2, len(parts), peers)),
            pltpu.SemaphoreType.DMA((2, len(parts), peers)),
        ],
        compiler_params=pltpu.CompilerParams(
            collective_id=0, has_side_effects=True, vmem_limit_bytes=40 * 1024 * 1024
        ),
        name="step",
    )(*[pltpu.with_memory_space_constraint(a, pltpu.HBM) for a in operands])


def solution(mesh):
    placed = (
        P(None, None, "dom"),
        P(None, None, "dom"),
        P(None, None, "dom"),
        P(None, None, None, "dom"),
        P(None, None, None, "dom"),
        P(None, "dom"),
        P(None, "dom"),
        P(None, "dom"),
    )
    return jax.shard_map(
        on_device, mesh=mesh, in_specs=placed, out_specs=P(None, None, "dom"), check_vma=False
    )
```

profile of v0, /device:TPU:0, one launch (start us, length us, event | category | flops | bytes accessed | tf_op | source)
XLA Modules:
  0.0 31.6 jit_solution(2136405159309310878)
XLA Ops:
  0.0 30.7 %step.1 = f32[20,8,1024]{2,1,0:T(8,128)S(1)} custom-call(f32[20,8,1024]{2,1,0:T(8,128)} %tracers_hbm.1, f32[3,8,1024]{2,1,0:T(8,128)} %flux_hbm.1, f32[3,2,1024]{2,1,0:T(2,128)} %bitcast.1, f32[2,3,8,1024]{3,2,1,0:T(8,128)} %own_hbm.1, f32[2,3,8,1024]{3,2,1,0:T(8,128)} %far_hbm.1, f32[8,1024]{1,0:T(8,128)} %inv_hbm.1, s32[3,1024]{1,0:T(4,128)} %near_hbm.1, ...), custom_call_target="tpu_custom_call" | custom-call | tf_op jit(solution)/shard_map/step/pallas_call | solution.py:285
  30.7 0.8 %copy.10 = f32[20,8,1024]{2,1,0:T(8,128)} copy(f32[20,8,1024]{2,1,0:T(8,128)S(1)} %step.1) | data formatting | bytes 1310720
where the time goes:
time: 31.9 us; the launch traced here: 31.6 us
  Pallas kernels  30.7 us (96%)
  local copies, waits for them, and re-layouts  0.84 us (3%)
    pallas_call x1, Pallas kernels, on_device(): pl.pallas_call(functools.partial(kernel, parts), out_shape=jax.ShapeDtype...  30.7 us
    unnamed x1, local copies, waits for them, and re-layouts  0.84 us

commit v1 on v0

--- a/solution.py
+++ b/solution.py
@@ -14,6 +14,14 @@
 
 def peer_shift(peer_slot):
     return (peer_slot // 2 + 1) * (1 - 2 * (peer_slot % 2))
+
+
+def wrap(position, devices):
+    return lax.rem(position + devices, devices)
+
+
+def leading(me):
+    return 0
 
 
 def lanes(block, width):
@@ -60,6 +68,7 @@
     halo_g,
     send_sem,
     recv_sem,
+    top_sem,
 ):
     tracer_count, level_count, cells = tracers.shape
     rows = tracer_count * level_count
@@ -67,14 +76,22 @@
     ext = cells + peers * halo
     me = lax.axis_index("dom")
     devices = lax.axis_size("dom")
-    target = [lax.rem(me + peer_shift(p) + devices, devices) for p in range(peers)]
+    lead = leading(me)
     f32, bf16 = jnp.float32, jnp.bfloat16
-    order = [p for q in (1, 2, 0) for p in range(peers) if p // 2 == q]
-    order += [p for p in range(peers) if p not in order]
+    reach = peers // 2
+    order = [q for q in (1, 2, 0) if q < reach] + list(range(3, reach))
 
     barrier = pltpu.get_barrier_semaphore()
     for p in range(peers):
-        pl.semaphore_signal(barrier, inc=1, device_id=(target[p],), device_id_type=MESH)
+        to = me + peer_shift(p)
+
+        @pl.when(to < devices)
+        def _():
+            pl.semaphore_signal(
+                barrier, inc=1, device_id=(wrap(to, devices),), device_id_type=MESH
+            )
+
+    below = sum([jnp.where(me + peer_shift(p) < 0, 1, 0) for p in range(peers)])
 
     pairs = (
         (send_hbm, send_cells),
@@ -86,15 +103,34 @@
         (far_hbm, far_off),
         (inv_hbm, inv_mass),
     )
+    early = sum(parts[0]) // level_count
+    soon, rest = pl.ds(0, early), pl.ds(early, tracer_count - early)
+    late = pltpu.make_async_copy(
+        tracers_hbm.at[rest], tracers.at[rest], load_sem.at[len(pairs)]
+    )
+    pairs = pairs[:1] + ((tracers_hbm.at[soon], tracers.at[soon]),) + pairs[2:]
     loads = [pltpu.make_async_copy(a, b, load_sem.at[i]) for i, (a, b) in enumerate(pairs)]
-    for load in loads:
+    for load in loads[:2] + [late] + loads[2:]:
         load.start()
     loads[0].wait()
 
-    for p in range(peers):
-        index = jnp.broadcast_to(send_cells[p : p + 1, :], (cells, halo))
-        equal = lax.broadcasted_iota(jnp.int32, (cells, halo), 0) == index
-        send_hot[:, p * halo : (p + 1) * halo] = jnp.where(equal, 1.0, 0.0).astype(bf16)
+    row = lax.broadcasted_iota(jnp.int32, (16, 128), 0).astype(jnp.int16)
+    one, zero = jnp.ones((16, 128), bf16), jnp.zeros((16, 128), bf16)
+
+    def match(table, count, width, dest, height):
+        for j in range(count):
+
+            def build(b, carry):
+                index = jnp.broadcast_to(table[j : j + 1, lanes(b, 128)], (16, 128))
+                index = index.astype(jnp.int16) - row
+                cols = pl.ds(pl.multiple_of(j * width + b * 128, 128), 128)
+                for r in range(0, height, 16):
+                    dest[r : r + 16, cols] = jnp.where(index == jnp.int16(r), one, zero)
+                return carry
+
+            lax.fori_loop(0, width // 128, build, 0)
+
+    match(send_cells, peers, halo, send_hot, cells)
 
     loads[1].wait()
 
@@ -109,20 +145,47 @@
 
         lax.fori_loop(0, count // 16, step, 0)
 
-    def copies(kind, c):
+    def copy_of(kind, c, p, to):
         src, dst = (value_out, value_in) if kind == 0 else (grad_out, grad_in)
         start, count = [(1 + kind) * v for v in parts[c]]
-        return [
-            pltpu.make_async_remote_copy(
-                src_ref=src.at[p, pl.ds(start, count)],
-                dst_ref=dst.at[p, pl.ds(start, count)],
-                send_sem=send_sem.at[kind, c, p],
-                recv_sem=recv_sem.at[kind, c, p],
-                device_id=(target[p],),
-                device_id_type=MESH,
-            )
-            for p in order
-        ]
+        return pltpu.make_async_remote_copy(
+            src_ref=src.at[p, pl.ds(start, count)],
+            dst_ref=dst.at[p, pl.ds(start, count)],
+            send_sem=send_sem.at[kind],
+            recv_sem=recv_sem.at[kind, c],
+            device_id=(wrap(to, devices),),
+            device_id_type=MESH,
+        )
+
+    def all_of(kind, start, count, c):
+        src, dst = (value_out, value_in) if kind == 0 else (grad_out, grad_in)
+        return pltpu.make_async_remote_copy(
+            src_ref=src.at[:, pl.ds((1 + kind) * start, (1 + kind) * count)],
+            dst_ref=dst.at[:, pl.ds((1 + kind) * start, (1 + kind) * count)],
+            send_sem=send_sem.at[kind],
+            recv_sem=recv_sem.at[kind, c],
+            device_id=(wrap(me + 1, devices),),
+            device_id_type=MESH,
+        )
+
+    def send(kind, c, wanted):
+        for side in range(2):
+            bit = lead if side == 0 else 1 - lead
+            for q in order:
+                to = me + (q + 1) * (1 - 2 * bit)
+                pl.when(wanted(to))(copy_of(kind, c, 2 * q + bit, to).start)
+
+    def above_ground(to):
+        return to >= 0
+
+    def under_ground(to):
+        return to < 0
+
+    def late_gradient(to):
+        return jnp.logical_or(to < 0, jnp.logical_and(top, to < devices))
+
+    def soon_gradient(to):
+        return jnp.logical_not(late_gradient(to))
 
     def pack(terms, dest, start, count):
         for p in range(0, peers, 2):
@@ -135,7 +198,7 @@
             for q in range(2):
                 dest[p + q, pl.ds(start, count), :] = part[:, q * halo : (q + 1) * halo]
 
-    def local(terms, dest, scale):
+    def local(terms, dest, scale, first, last):
         def step(b, carry):
             cols = lanes(b, WIDTH)
             part = jnp.dot(terms[...], hot[:cells, cols], preferred_element_type=f32)
@@ -147,7 +210,7 @@
                 )
             return carry
 
-        lax.fori_loop(0, 3 * cells // WIDTH, step, 0)
+        lax.fori_loop(first, last, step, 0)
 
     def remote(arrived, terms, dest, start, count):
         for p in range(peers):
@@ -217,55 +280,87 @@
         lax.fori_loop(0, per // level_count, step, 0)
 
     count_parts = len(parts)
-    for part in parts:
-        split_x(*part)
-    whole = jnp.dot(low_x[...], send_hot[...], preferred_element_type=f32)
-    for start, count in parts:
-        part = whole[2 * start : 2 * start + count] + whole[2 * start + count : 2 * (start + count)]
-        for p in range(peers):
-            value_out[p, start : start + count, :] = part[:, p * halo : (p + 1) * halo]
-    pl.semaphore_wait(barrier, peers)
-    for c in range(count_parts):
-        for copy in copies(0, c):
-            copy.start()
+    def pack_x(first, last):
+        start, stop = parts[first][0], sum(parts[last])
+        for part in parts[first : last + 1]:
+            split_x(*part)
+        whole = jnp.dot(
+            low_x[2 * start : 2 * stop, :],
+            send_hot[:, : peers * halo],
+            preferred_element_type=f32,
+        )
+        for begin, count in parts[first : last + 1]:
+            at = 2 * (begin - start)
+            part = whole[at : at + count] + whole[at + count : at + 2 * count]
+            for p in range(peers):
+                value_out[p, begin : begin + count, :] = part[:, p * halo : (p + 1) * halo]
+
+    top = me + reach >= devices
+
+    def enter():
+        pl.semaphore_wait(barrier, peers - below)
+
+    @pl.when(top)
+    def _():
+        enter()
+        for q in range(reach):
+            to = me + q + 1
+
+            @pl.when(to >= devices)
+            def _():
+                pl.semaphore_signal(
+                    top_sem, inc=1, device_id=(wrap(to, devices),), device_id_type=MESH
+                )
+
+    pack_x(0, 0)
+    interior = jnp.logical_not(jnp.logical_or(top, below > 0))
+    pl.when(interior)(enter)
+
+    @pl.when(below == 0)
+    def _():
+        send(0, 0, above_ground)
+
+    late.wait()
+    pack_x(1, count_parts - 1)
+
+    @pl.when(below > 0)
+    def _():
+        enter()
+        send(0, 0, above_ground)
+
+    for c in range(1, count_parts):
+        send(0, c, above_ground)
     loads[2].wait()
-    for j in range(3):
-
-        def build(b, carry):
-            cols = lanes(b, 128)
-            index = jnp.broadcast_to(near[j : j + 1, cols], (ext, 128))
-            equal = lax.broadcasted_iota(jnp.int32, (ext, 128), 0) == index
-            hot[:, pl.ds(pl.multiple_of(j * cells + b * 128, 128), 128)] = jnp.where(
-                equal, 1.0, 0.0
-            ).astype(bf16)
-            return carry
-
-        lax.fori_loop(0, cells // 128, build, 0)
-
-    local(low_x, beside, 1)
+    match(near, 3, cells, hot, ext)
     loads[3].wait()
+    local(low_x, beside, 1, 0, 1)
+
+    @pl.when(below > 0)
+    def _():
+        pl.semaphore_wait(top_sem, below)
+        for c in range(count_parts):
+            send(0, c, under_ground)
+
+    local(low_x, beside, 1, 1, 3 * cells // WIDTH)
     for c in range(count_parts):
         start, count = parts[c]
-        for copy in copies(0, c):
-            copy.wait_recv()
+        all_of(0, start, count, c).wait_recv()
         remote(value_in, halo_x, beside, start, count)
         gradient(start, count)
         pack(low_g, grad_out, 2 * start, 2 * count)
-        for copy in copies(1, c):
-            copy.start()
-    local(low_g, far, 2)
+        send(1, c, soon_gradient)
+    for c in range(count_parts):
+        send(1, c, late_gradient)
+    local(low_g, far, 2, 0, 3 * cells // WIDTH)
     for load in loads[4:]:
         load.wait()
     for c in range(count_parts):
         start, count = parts[c]
-        for copy in copies(1, c):
-            copy.wait_recv()
+        all_of(1, start, count, c).wait_recv()
         remote(grad_in, halo_g, far, 2 * start, 2 * count)
         finish(start, count)
     for kind in range(2):
-        for c in range(count_parts):
-            for copy in copies(kind, c):
-                copy.wait_send()
+        all_of(kind, 0, rows, 0).wait_send()
 
 
 def on_device(tracers, flux, lsq, own_off, far_off, inv_mass, near, send_cells):
@@ -289,9 +384,9 @@
         out_specs=pl.BlockSpec(memory_space=pltpu.VMEM),
         scratch_shapes=[pltpu.VMEM(a.shape, a.dtype) for a in operands]
         + [
-            pltpu.SemaphoreType.DMA((8,)),
-            pltpu.VMEM((ext, 3 * cells), bf16),
-            pltpu.VMEM((cells, peers * halo), bf16),
+            pltpu.SemaphoreType.DMA((9,)),
+            pltpu.VMEM((ext, 3 * cells + 128), bf16),
+            pltpu.VMEM((cells, peers * halo + 128), bf16),
             pltpu.VMEM((2 * rows, cells), bf16),
             pltpu.VMEM((4 * rows, cells), bf16),
             pltpu.VMEM((2, rows, cells), f32),
@@ -303,8 +398,9 @@
             pltpu.VMEM((peers, 2 * rows, halo), f32),
             pltpu.VMEM((2 * per, peers * halo), bf16),
             pltpu.VMEM((4 * per, peers * halo), bf16),
-            pltpu.SemaphoreType.DMA((2, len(parts), peers)),
-            pltpu.SemaphoreType.DMA((2, len(parts), peers)),
+            pltpu.SemaphoreType.DMA((2,)),
+            pltpu.SemaphoreType.DMA((2, len(parts))),
+            pltpu.SemaphoreType.REGULAR,
         ],
         compiler_params=pltpu.CompilerParams(
             collective_id=0, has_side_effects=True, vmem_limit_bytes=40 * 1024 * 1024

time: 31.9 us -> 30.7 us (0.962)
  Pallas kernels: 30.7 us -> 29.7 us
    pallas_call x1, Pallas kernels: 30.7 us -> 29.7 us  [on_device(): pl.pallas_call(functools.partial(kernel, parts), out_shape=jax.ShapeDtype...]
where the time goes in v1:
time: 30.7 us; the launch traced here: 30.6 us
  Pallas kernels  29.7 us (97%)
  local copies, waits for them, and re-layouts  0.84 us (3%)
    pallas_call x1, Pallas kernels, on_device(): pl.pallas_call(functools.partial(kernel, parts), out_shape=jax.ShapeDtype...  29.7 us
    unnamed x1, local copies, waits for them, and re-layouts  0.84 us

profile of v1, /device:TPU:0, one launch (start us, length us, event | category | flops | bytes accessed | tf_op | source)
XLA Modules:
  0.0 30.6 jit_solution(12090433693484010947)
XLA Ops:
  0.0 29.7 %step.1 = f32[20,8,1024]{2,1,0:T(8,128)S(1)} custom-call(f32[20,8,1024]{2,1,0:T(8,128)} %tracers_hbm.1, f32[3,8,1024]{2,1,0:T(8,128)} %flux_hbm.1, f32[3,2,1024]{2,1,0:T(2,128)} %bitcast.1, f32[2,3,8,1024]{3,2,1,0:T(8,128)} %own_hbm.1, f32[2,3,8,1024]{3,2,1,0:T(8,128)} %far_hbm.1, f32[8,1024]{1,0:T(8,128)} %inv_hbm.1, s32[3,1024]{1,0:T(4,128)} %near_hbm.1, ...), custom_call_target="tpu_custom_call" | custom-call | tf_op jit(solution)/shard_map/step/pallas_call | solution.py:380
  29.7 0.8 %copy.10 = f32[20,8,1024]{2,1,0:T(8,128)} copy(f32[20,8,1024]{2,1,0:T(8,128)S(1)} %step.1) | data formatting | bytes 1310720

commit v2 on v1

--- a/solution.py
+++ b/solution.py
@@ -8,8 +8,9 @@
 from jax.sharding import PartitionSpec as P
 
 MESH = pl.DeviceIdType.MESH
-PARTS = (2, 3, 3, 2)
+PARTS = (2, 2, 3, 2, 1)
 WIDTH = 1536
+ONE_HOT = jnp.float8_e4m3fn
 
 
 def peer_shift(peer_slot):
@@ -26,6 +27,12 @@
 
 def lanes(block, width):
     return pl.ds(pl.multiple_of(block * width, width), width)
+
+
+def pick(terms, one_hot):
+    return lax.dot_general(
+        terms, one_hot, (((1,), (0,)), ((), ())), preferred_element_type=jnp.float32
+    )
 
 
 def split(value):
@@ -112,20 +119,38 @@
     loads = [pltpu.make_async_copy(a, b, load_sem.at[i]) for i, (a, b) in enumerate(pairs)]
     for load in loads[:2] + [late] + loads[2:]:
         load.start()
+    top = me + reach >= devices
+
+    def enter():
+        pl.semaphore_wait(barrier, peers - below)
+
+    @pl.when(top)
+    def _():
+        enter()
+        for q in range(reach):
+            to = me + q + 1
+
+            @pl.when(to >= devices)
+            def _():
+                pl.semaphore_signal(
+                    top_sem.at[q], inc=1, device_id=(wrap(to, devices),), device_id_type=MESH
+                )
+
     loads[0].wait()
 
-    row = lax.broadcasted_iota(jnp.int32, (16, 128), 0).astype(jnp.int16)
-    one, zero = jnp.ones((16, 128), bf16), jnp.zeros((16, 128), bf16)
+    row = lax.broadcasted_iota(jnp.int32, (32, 128), 0).astype(jnp.int16)
+    one, zero = jnp.ones((32, 128), bf16), jnp.zeros((32, 128), bf16)
 
     def match(table, count, width, dest, height):
         for j in range(count):
 
             def build(b, carry):
-                index = jnp.broadcast_to(table[j : j + 1, lanes(b, 128)], (16, 128))
+                index = jnp.broadcast_to(table[j : j + 1, lanes(b, 128)], (32, 128))
                 index = index.astype(jnp.int16) - row
                 cols = pl.ds(pl.multiple_of(j * width + b * 128, 128), 128)
-                for r in range(0, height, 16):
-                    dest[r : r + 16, cols] = jnp.where(index == jnp.int16(r), one, zero)
+                for r in range(0, height, 32):
+                    hit = jnp.where(index == jnp.int16(r), one, zero)
+                    dest[r : r + 32, cols] = hit.astype(dest.dtype)
                 return carry
 
             lax.fori_loop(0, width // 128, build, 0)
@@ -182,17 +207,16 @@
         return to < 0
 
     def late_gradient(to):
-        return jnp.logical_or(to < 0, jnp.logical_and(top, to < devices))
+        last = me + reach + 1 >= devices
+        return (to < 0) | (top & (to < devices)) | (last & (to == me - reach))
 
     def soon_gradient(to):
         return jnp.logical_not(late_gradient(to))
 
     def pack(terms, dest, start, count):
         for p in range(0, peers, 2):
-            part = jnp.dot(
-                terms[pl.ds(2 * start, 2 * count), :],
-                send_hot[:, p * halo : (p + 2) * halo],
-                preferred_element_type=f32,
+            part = pick(
+                terms[pl.ds(2 * start, 2 * count), :], send_hot[:, p * halo : (p + 2) * halo]
             )
             part = part[:count] + part[count:]
             for q in range(2):
@@ -201,7 +225,7 @@
     def local(terms, dest, scale, first, last):
         def step(b, carry):
             cols = lanes(b, WIDTH)
-            part = jnp.dot(terms[...], hot[:cells, cols], preferred_element_type=f32)
+            part = pick(terms[...], hot[:cells, cols])
             for start, count in parts:
                 start, count = scale * start, scale * count
                 s = 2 * start
@@ -220,9 +244,7 @@
 
         def step(b, carry):
             cols = lanes(b, 2 * WIDTH)
-            part = jnp.dot(
-                terms[: 2 * count, :], hot[cells:ext, cols], preferred_element_type=f32
-            )
+            part = pick(terms[: 2 * count, :], hot[cells:ext, cols])
             dest[start : start + count, cols] += part[:count] + part[count:]
             return carry
 
@@ -284,33 +306,12 @@
         start, stop = parts[first][0], sum(parts[last])
         for part in parts[first : last + 1]:
             split_x(*part)
-        whole = jnp.dot(
-            low_x[2 * start : 2 * stop, :],
-            send_hot[:, : peers * halo],
-            preferred_element_type=f32,
-        )
+        whole = pick(low_x[2 * start : 2 * stop, :], send_hot[:, : peers * halo])
         for begin, count in parts[first : last + 1]:
             at = 2 * (begin - start)
             part = whole[at : at + count] + whole[at + count : at + 2 * count]
             for p in range(peers):
                 value_out[p, begin : begin + count, :] = part[:, p * halo : (p + 1) * halo]
-
-    top = me + reach >= devices
-
-    def enter():
-        pl.semaphore_wait(barrier, peers - below)
-
-    @pl.when(top)
-    def _():
-        enter()
-        for q in range(reach):
-            to = me + q + 1
-
-            @pl.when(to >= devices)
-            def _():
-                pl.semaphore_signal(
-                    top_sem, inc=1, device_id=(wrap(to, devices),), device_id_type=MESH
-                )
 
     pack_x(0, 0)
     interior = jnp.logical_not(jnp.logical_or(top, below > 0))
@@ -337,8 +338,15 @@
 
     @pl.when(below > 0)
     def _():
-        pl.semaphore_wait(top_sem, below)
-        for c in range(count_parts):
+        for q in order[::-1]:
+            to = me - q - 1
+
+            @pl.when(to < 0)
+            def _():
+                pl.semaphore_wait(top_sem.at[q], 1)
+                copy_of(0, 0, 2 * q + 1, to).start()
+
+        for c in range(1, count_parts):
             send(0, c, under_ground)
 
     local(low_x, beside, 1, 1, 3 * cells // WIDTH)
@@ -385,8 +393,8 @@
         scratch_shapes=[pltpu.VMEM(a.shape, a.dtype) for a in operands]
         + [
             pltpu.SemaphoreType.DMA((9,)),
-            pltpu.VMEM((ext, 3 * cells + 128), bf16),
-            pltpu.VMEM((cells, peers * halo + 128), bf16),
+            pltpu.VMEM((ext, 3 * cells + 128), ONE_HOT),
+            pltpu.VMEM((cells, peers * halo + 128), ONE_HOT),
             pltpu.VMEM((2 * rows, cells), bf16),
             pltpu.VMEM((4 * rows, cells), bf16),
             pltpu.VMEM((2, rows, cells), f32),
@@ -400,7 +408,7 @@
             pltpu.VMEM((4 * per, peers * halo), bf16),
             pltpu.SemaphoreType.DMA((2,)),
             pltpu.SemaphoreType.DMA((2, len(parts))),
-            pltpu.SemaphoreType.REGULAR,
+            pltpu.SemaphoreType.REGULAR((peers // 2,)),
         ],
         compiler_params=pltpu.CompilerParams(
             collective_id=0, has_side_effects=True, vmem_limit_bytes=40 * 1024 * 1024

time: 30.7 us -> 28.4 us (0.925)
  Pallas kernels: 29.7 us -> 27.4 us
    pallas_call x1, Pallas kernels: 29.7 us -> 27.4 us  [on_device(): pl.pallas_call(functools.partial(kernel, parts), out_shape=jax.ShapeDtype...]
where the time goes in v2:
time: 28.4 us; the launch traced here: 28.2 us
  Pallas kernels  27.4 us (96%)
  local copies, waits for them, and re-layouts  0.84 us (3%)
    pallas_call x1, Pallas kernels, on_device(): pl.pallas_call(functools.partial(kernel, parts), out_shape=jax.ShapeDtype...  27.4 us
    unnamed x1, local copies, waits for them, and re-layouts  0.84 us

profile of v2, /device:TPU:0, one launch (start us, length us, event | category | flops | bytes accessed | tf_op | source)
XLA Modules:
  0.0 28.2 jit_solution(7537057059299041079)
XLA Ops:
  0.0 27.4 %step.1 = f32[20,8,1024]{2,1,0:T(8,128)S(1)} custom-call(f32[20,8,1024]{2,1,0:T(8,128)} %tracers_hbm.1, f32[3,8,1024]{2,1,0:T(8,128)} %flux_hbm.1, f32[3,2,1024]{2,1,0:T(2,128)} %bitcast.1, f32[2,3,8,1024]{3,2,1,0:T(8,128)} %own_hbm.1, f32[2,3,8,1024]{3,2,1,0:T(8,128)} %far_hbm.1, f32[8,1024]{1,0:T(8,128)} %inv_hbm.1, s32[3,1024]{1,0:T(4,128)} %near_hbm.1, ...), custom_call_target="tpu_custom_call" | custom-call | tf_op jit(solution)/shard_map/step/pallas_call | solution.py:388
  27.4 0.8 %copy.10 = f32[20,8,1024]{2,1,0:T(8,128)} copy(f32[20,8,1024]{2,1,0:T(8,128)S(1)} %step.1) | data formatting | bytes 1310720

commit v3 on v2

--- a/solution.py
+++ b/solution.py
@@ -8,7 +8,7 @@
 from jax.sharding import PartitionSpec as P
 
 MESH = pl.DeviceIdType.MESH
-PARTS = (2, 2, 3, 2, 1)
+PARTS = (2, 2, 2, 2, 1, 1)
 WIDTH = 1536
 ONE_HOT = jnp.float8_e4m3fn
 
@@ -19,10 +19,6 @@
 
 def wrap(position, devices):
     return lax.rem(position + devices, devices)
-
-
-def leading(me):
-    return 0
 
 
 def lanes(block, width):
@@ -83,7 +79,6 @@
     ext = cells + peers * halo
     me = lax.axis_index("dom")
     devices = lax.axis_size("dom")
-    lead = leading(me)
     f32, bf16 = jnp.float32, jnp.bfloat16
     reach = peers // 2
     order = [q for q in (1, 2, 0) if q < reach] + list(range(3, reach))
@@ -194,24 +189,20 @@
         )
 
     def send(kind, c, wanted):
-        for side in range(2):
-            bit = lead if side == 0 else 1 - lead
+        for bit in range(2):
             for q in order:
                 to = me + (q + 1) * (1 - 2 * bit)
-                pl.when(wanted(to))(copy_of(kind, c, 2 * q + bit, to).start)
+                copy = copy_of(kind, c, 2 * q + bit, to)
+                if wanted is None:
+                    copy.start()
+                else:
+                    pl.when(wanted(to))(copy.start)
 
     def above_ground(to):
         return to >= 0
 
     def under_ground(to):
         return to < 0
-
-    def late_gradient(to):
-        last = me + reach + 1 >= devices
-        return (to < 0) | (top & (to < devices)) | (last & (to == me - reach))
-
-    def soon_gradient(to):
-        return jnp.logical_not(late_gradient(to))
 
     def pack(terms, dest, start, count):
         for p in range(0, peers, 2):
@@ -356,9 +347,7 @@
         remote(value_in, halo_x, beside, start, count)
         gradient(start, count)
         pack(low_g, grad_out, 2 * start, 2 * count)
-        send(1, c, soon_gradient)
-    for c in range(count_parts):
-        send(1, c, late_gradient)
+        send(1, c, None)
     local(low_g, far, 2, 0, 3 * cells // WIDTH)
     for load in loads[4:]:
         load.wait()

time: 28.4 us -> 28.3 us (level)
  no operation moved by 1% of the time
where the time goes in v3:
time: 28.3 us; the launch traced here: 28.2 us
  Pallas kernels  27.3 us (96%)
  local copies, waits for them, and re-layouts  0.84 us (3%)
    pallas_call x1, Pallas kernels, on_device(): pl.pallas_call(functools.partial(kernel, parts), out_shape=jax.ShapeDtype...  27.3 us
    unnamed x1, local copies, waits for them, and re-layouts  0.84 us

profile of v3, /device:TPU:0, one launch (start us, length us, event | category | flops | bytes accessed | tf_op | source)
XLA Modules:
  0.0 28.2 jit_solution(4896072732031452840)
XLA Ops:
  0.0 27.3 %step.1 = f32[20,8,1024]{2,1,0:T(8,128)S(1)} custom-call(f32[20,8,1024]{2,1,0:T(8,128)} %tracers_hbm.1, f32[3,8,1024]{2,1,0:T(8,128)} %flux_hbm.1, f32[3,2,1024]{2,1,0:T(2,128)} %bitcast.1, f32[2,3,8,1024]{3,2,1,0:T(8,128)} %own_hbm.1, f32[2,3,8,1024]{3,2,1,0:T(8,128)} %far_hbm.1, f32[8,1024]{1,0:T(8,128)} %inv_hbm.1, s32[3,1024]{1,0:T(4,128)} %near_hbm.1, ...), custom_call_target="tpu_custom_call" | custom-call | tf_op jit(solution)/shard_map/step/pallas_call | solution.py:377
  27.3 0.8 %copy.10 = f32[20,8,1024]{2,1,0:T(8,128)} copy(f32[20,8,1024]{2,1,0:T(8,128)S(1)} %step.1) | data formatting | bytes 1310720

commit v4 on v3

--- a/solution.py
+++ b/solution.py
@@ -205,13 +205,10 @@
         return to < 0
 
     def pack(terms, dest, start, count):
-        for p in range(0, peers, 2):
-            part = pick(
-                terms[pl.ds(2 * start, 2 * count), :], send_hot[:, p * halo : (p + 2) * halo]
-            )
-            part = part[:count] + part[count:]
-            for q in range(2):
-                dest[p + q, pl.ds(start, count), :] = part[:, q * halo : (q + 1) * halo]
+        part = pick(terms[pl.ds(2 * start, 2 * count), :], send_hot[:, : peers * halo])
+        part = part[:count] + part[count:]
+        for p in range(peers):
+            dest[p, pl.ds(start, count), :] = part[:, p * halo : (p + 1) * halo]
 
     def local(terms, dest, scale, first, last):
         def step(b, carry):

time: 28.3 us -> 28.3 us (level)
  no operation moved by 1% of the time
where the time goes in v4:
time: 28.3 us; the launch traced here: 28.2 us
  Pallas kernels  27.3 us (96%)
  local copies, waits for them, and re-layouts  0.84 us (3%)
    pallas_call x1, Pallas kernels, on_device(): pl.pallas_call(functools.partial(kernel, parts), out_shape=jax.ShapeDtype...  27.3 us
    unnamed x1, local copies, waits for them, and re-layouts  0.84 us

profile of v4, /device:TPU:0, one launch (start us, length us, event | category | flops | bytes accessed | tf_op | source)
XLA Modules:
  0.0 28.2 jit_solution(5714982642506666438)
XLA Ops:
  0.0 27.3 %step.1 = f32[20,8,1024]{2,1,0:T(8,128)S(1)} custom-call(f32[20,8,1024]{2,1,0:T(8,128)} %tracers_hbm.1, f32[3,8,1024]{2,1,0:T(8,128)} %flux_hbm.1, f32[3,2,1024]{2,1,0:T(2,128)} %bitcast.1, f32[2,3,8,1024]{3,2,1,0:T(8,128)} %own_hbm.1, f32[2,3,8,1024]{3,2,1,0:T(8,128)} %far_hbm.1, f32[8,1024]{1,0:T(8,128)} %inv_hbm.1, s32[3,1024]{1,0:T(4,128)} %near_hbm.1, ...), custom_call_target="tpu_custom_call" | custom-call | tf_op jit(solution)/shard_map/step/pallas_call | solution.py:374
  27.3 0.8 %copy.10 = f32[20,8,1024]{2,1,0:T(8,128)} copy(f32[20,8,1024]{2,1,0:T(8,128)S(1)} %step.1) | data formatting | bytes 1310720
